TPU v7x, 32 devices: a whole 2x2x4 slice. The times are simulated.
32 devices in a mesh: row: 4 (over y, core), col: 8 (over z, x).
Axes of the slice: x: 2, y: 2, z: 4, core: 2. Of those that a mesh axis runs over, the one named last changes fastest.
Arguments:
- lhat: float32 [256, 256, 256], P(('row', 'col')), may hold values from -0.375 to 0.375
- ainv_anc: float32 [256, 256, 256], P(('row', 'col')), may hold values from -2.5 to 2.5
- diag_inv: float32 [8, 256, 256], P('col', 'row'), may hold values from -0.6 to 2, as said below
- targets: int32 [256, 1], P(('row', 'col')), may hold values from 0 to 7
Outputs:
- diag_blocks: float32 [8, 256, 256], P('col', 'row')
Inputs may be any that keep to these rules, and one draw needn't show every extreme that they name: `diag_inv`: each block is lower triangular with its diagonal entries between 0.5 and 2.
All inputs are finite; a program needn't handle non-finite values.
Results may differ from a plain program's by a relative error of at most 0.0003.
Values sent between devices are 32-bit elements; how exact they have to be, the bound alone decides.
A program may use at most 64 MiB of HBM per device.

v0:
```python
import functools

import jax
import jax.numpy as jnp
from jax import lax
from jax.experimental import pallas as pl
from jax.experimental.pallas import tpu as pltpu
from jax.sharding import PartitionSpec as P

MESH = pl.DeviceIdType.MESH
DN = (((0,), (0,)), ((), ()))


def gram_dot(a, b):
    a_hi = a.astype(jnp.bfloat16)
    a_lo = (a - a_hi.astype(jnp.float32)).astype(jnp.bfloat16)
    b_hi = b.astype(jnp.bfloat16)
    b_lo = (b - b_hi.astype(jnp.float32)).astype(jnp.bfloat16)
    left = jnp.concatenate([a_hi, a_lo, a_hi], axis=0)
    right = jnp.concatenate([b_hi, b_hi, b_lo], axis=0)
    return lax.dot_general(left, right, DN, preferred_element_type=jnp.float32)


def kernel(
    dims,
    lhat, ainv, diag, targets_in, out,
    targets, lbuf, abuf, dbuf, prod, send0, own0, recv0, send1a, send1b, recv1a, recv1b,
    sum2a, sum2b, recv2a, recv2b, sum3, recv3,
    load_sem, d_sem, t_sem, s0, r0, s1a, r1a, s1b, r1b, s2a, r2a, s2b, r2b, s3, r3,
):
    yn, zn, slots, share, width = dims
    half = width // 2
    row, col = lax.axis_index("row"), lax.axis_index("col")
    y, c = lax.div(row, 2), lax.rem(row, 2)
    z, x = lax.div(col, 2), lax.rem(col, 2)

    def dev(y_, c_, z_, x_):
        return {"row": y_ * 2 + c_, "col": z_ * 2 + x_}

    shifts = [zn // 2] + [d for d in range(1, zn) if d != zn // 2] if zn > 1 else []
    order = shifts + [0]
    core_peer = dev(y, 1 - c, z, x)
    x_peer = dev(y, c, z, 1 - x)
    y_ids = [lax.rem(y + d, yn) for d in range(1, yn)]
    y_peers = [dev(i, c, z, x) for i in y_ids]
    z_peers = [dev(y, c, lax.rem(z + d, zn), x) for d in shifts]
    peers = [core_peer, x_peer] + y_peers + z_peers

    t_load = pltpu.make_async_copy(targets_in, targets, t_sem)
    t_load.start()
    loads = []
    for s in range(slots):
        pair = (
            pltpu.make_async_copy(lhat.at[s], lbuf.at[s], load_sem.at[s, 0]),
            pltpu.make_async_copy(ainv.at[s], abuf.at[s], load_sem.at[s, 1]),
        )
        for copy in pair:
            copy.start()
        loads.append(pair)
    d_load = pltpu.make_async_copy(diag.at[0], dbuf, d_sem)
    d_load.start()

    barrier = pltpu.get_barrier_semaphore()
    for peer in peers:
        pl.semaphore_signal(barrier, inc=1, device_id=peer, device_id_type=MESH)

    for s in range(slots):
        for copy in loads[s]:
            copy.wait()
        prod[s] = gram_dot(lbuf[s], abuf[s]).reshape(yn, 2, share, width)
    d_load.wait()
    t_load.wait()
    prod[slots] = gram_dot(dbuf[...], dbuf[...]).reshape(yn, 2, share, width)

    def segment(o, side, dest):
        zd = lax.rem(z + order[o], zn)
        for xi in range(2):
            k = zd * 2 + xi
            weights = [jnp.where(targets[0, s] == k, -1.0, 0.0) for s in range(slots)]
            weights.append(jnp.where(col == k, 1.0, 0.0))

            def body(yo, carry):
                for h in range(2):
                    lanes = slice(h * half, (h + 1) * half)
                    total = weights[0] * prod[0, yo, side, :, lanes]
                    for s in range(1, slots + 1):
                        total = total + weights[s] * prod[s, yo, side, :, lanes]
                    dest[o, h, xi, yo] = total
                return carry

            lax.fori_loop(0, yn, body, 0)

    def remote(src, dst, send, recv, peer):
        copy = pltpu.make_async_remote_copy(
            src_ref=src, dst_ref=dst, send_sem=send, recv_sem=recv, device_id=peer, device_id_type=MESH
        )
        copy.start()
        return copy

    started = []
    copies0, copies1a, copies1b, copies2a, copies2b = {}, {}, {}, {}, {}
    copies3 = {}

    def stage0(o):
        copies0[o] = remote(send0.at[o], recv0.at[o], s0.at[o], r0.at[o], core_peer)
        started.append(copies0[o])

    def stage1(o):
        copies0[o].wait_recv()
        send1a[o] = own0[o, 0, 1 - x] + recv0[o, 0, 1 - x]
        for i, yo in enumerate(y_ids):
            for xi in range(2):
                send1b[o, i, xi] = own0[o, 1, xi, yo] + recv0[o, 1, xi, yo]
        copies1a[o] = remote(send1a.at[o], recv1a.at[o], s1a.at[o], r1a.at[o], x_peer)
        copies1b[o] = [
            remote(send1b.at[o, i], recv1b.at[o, i], s1b.at[o, i], r1b.at[o, i], peer)
            for i, peer in enumerate(y_peers)
        ]
        started.extend([copies1a[o]] + copies1b[o])

    def stage2(o):
        copies1a[o].wait_recv()
        sum2a[o] = own0[o, 0, x] + recv0[o, 0, x] + recv1a[o]
        copies2a[o] = [
            remote(sum2a.at[o, yo], recv2a.at[o, i], s2a.at[o, i], r2a.at[o, i], peer)
            for i, (yo, peer) in enumerate(zip(y_ids, y_peers))
        ]
        for copy in copies1b[o]:
            copy.wait_recv()
        for xi in range(2):
            total = own0[o, 1, xi, y] + recv0[o, 1, xi, y]
            for i in range(yn - 1):
                total = total + recv1b[o, i, xi]
            sum2b[o, xi] = total
        copies2b[o] = remote(sum2b.at[o, 1 - x], recv2b.at[o], s2b.at[o], r2b.at[o], x_peer)
        started.extend(copies2a[o] + [copies2b[o]])

    def stage3(o):
        for copy in copies2a[o]:
            copy.wait_recv()
        total = sum2a[o, y]
        for i in range(yn - 1):
            total = total + recv2a[o, i]
        sum3[o, 0] = total
        if o < zn - 1:
            first = remote(sum3.at[o, 0], recv3.at[o, 0], s3.at[o, 0], r3.at[o, 0], z_peers[o])
        copies2b[o].wait_recv()
        sum3[o, 1] = sum2b[o, x] + recv2b[o]
        if o < zn - 1:
            second = remote(sum3.at[o, 1], recv3.at[o, 1], s3.at[o, 1], r3.at[o, 1], z_peers[o])
            copies3[o] = (first, second)
            started.extend(copies3[o])

    for o in range(zn):
        segment(o, 1 - c, send0)
        if o == 0:
            pl.semaphore_wait(barrier, len(peers))
        stage0(o)
    ahead, lag = 2, 2
    for step in range(zn + ahead + lag):
        if step < zn:
            segment(step, c, own0)
            stage1(step)
        if 0 <= step - ahead < zn:
            stage2(step - ahead)
        if 0 <= step - ahead - lag < zn:
            stage3(step - ahead - lag)

    totals = [sum3[zn - 1, h] for h in range(2)]
    for o in range(zn - 1):
        for h in range(2):
            copies3[o][h].wait_recv()
            totals[h] = totals[h] + recv3[o, h]
    for h in range(2):
        out[0, :, h * half:(h + 1) * half] = totals[h]
    for copy in started:
        copy.wait_send()


def on_device(lhat, ainv, diag, targets):
    rows, cols = lax.axis_size("row"), lax.axis_size("col")
    slots, width = lhat.shape[0], lhat.shape[2]
    height = lhat.shape[1]
    yn, zn, share = rows // 2, cols // 2, diag.shape[1]
    half = width // 2
    f32, dma = jnp.float32, pltpu.SemaphoreType.DMA
    tail = (share, half)
    scratch = [
        pltpu.SMEM((1, slots), jnp.int32),
        pltpu.VMEM((slots, height, width), f32),
        pltpu.VMEM((slots, height, width), f32),
        pltpu.VMEM((share, width), f32),
        pltpu.VMEM((slots + 1, yn, 2, share, width), f32),
        pltpu.VMEM((zn, 2, 2, yn) + tail, f32),
        pltpu.VMEM((zn, 2, 2, yn) + tail, f32),
        pltpu.VMEM((zn, 2, 2, yn) + tail, f32),
        pltpu.VMEM((zn, yn) + tail, f32),
        pltpu.VMEM((zn, yn - 1, 2) + tail, f32),
        pltpu.VMEM((zn, yn) + tail, f32),
        pltpu.VMEM((zn, yn - 1, 2) + tail, f32),
        pltpu.VMEM((zn, yn) + tail, f32),
        pltpu.VMEM((zn, 2) + tail, f32),
        pltpu.VMEM((zn, yn - 1) + tail, f32),
        pltpu.VMEM((zn,) + tail, f32),
        pltpu.VMEM((zn, 2) + tail, f32),
        pltpu.VMEM((zn - 1, 2) + tail, f32),
        dma((slots, 2)), dma, dma,
        dma((zn,)), dma((zn,)),
        dma((zn,)), dma((zn,)),
        dma((zn, yn - 1)), dma((zn, yn - 1)),
        dma((zn, yn - 1)), dma((zn, yn - 1)),
        dma((zn,)), dma((zn,)),
        dma((zn - 1, 2)), dma((zn - 1, 2)),
    ]
    return pl.pallas_call(
        functools.partial(kernel, (yn, zn, slots, share, width)),
        out_shape=pltpu.VMEM(diag.shape, f32),
        in_specs=[pl.BlockSpec(memory_space=pltpu.HBM)] * 4,
        out_specs=pl.BlockSpec(memory_space=pltpu.VMEM),
        scratch_shapes=scratch,
        compiler_params=pltpu.CompilerParams(
            collective_id=0, has_side_effects=True, vmem_limit_bytes=60 * 1024 * 1024
        ),
    )(lhat, ainv, diag, targets.T)


def solution(mesh):
    placed = (
        P(("row", "col"), None, None),
        P(("row", "col"), None, None),
        P("col", "row", None),
        P(("row", "col"), None),
    )
    return jax.shard_map(
        on_device, mesh=mesh, in_specs=placed, out_specs=P("col", "row", None), check_vma=False
    )
```

profile of v0, /device:TPU:0, one launch (start us, length us, event | category | flops | bytes accessed | tf_op | source)
XLA Modules:
  0.0 24.6 jit_solution(15211120145947052621)
XLA Ops:
  0.0 24.0 %shard_map.46 = f32[1,64,256]{2,1,0:T(8,128)S(1)} custom-call(f32[8,256,256]{2,1,0:T(8,128)} %lhat.1, f32[8,256,256]{2,1,0:T(8,128)} %ainv.1, f32[1,64,256]{2,1,0:T(8,128)} %diag.1, s32[1,8]{1,0:T(1,128)} %bitcast.1), custom_call_target="tpu_custom_call" | custom-call | tf_op jit(solution)/shard_map/pallas_call | solution.py:215
  24.0 0.6 %copy.6 = f32[1,64,256]{2,1,0:T(8,128)} copy(f32[1,64,256]{2,1,0:T(8,128)S(1)} %shard_map.46) | data formatting | bytes 131072
where the time goes:
time: 24.8 us; the launch traced here: 24.6 us
  Pallas kernels  24 us (97%)
  local copies, waits for them, and re-layouts  0.63 us (3%)
    pallas_call x1, Pallas kernels, on_device(): pl.pallas_call(functools.partial(kernel, (yn, zn, slots, share, width)),...  24 us
    unnamed x1, local copies, waits for them, and re-layouts  0.63 us

commit v1 on v0

--- a/solution.py
+++ b/solution.py
@@ -24,9 +24,9 @@
 def kernel(
     dims,
     lhat, ainv, diag, targets_in, out,
-    targets, lbuf, abuf, dbuf, prod, send0, own0, recv0, send1a, send1b, recv1a, recv1b,
+    targets, lbuf, abuf, dbuf, prod, cum, send0, recv0, send1a, send1b, recv1a, recv1b,
     sum2a, sum2b, recv2a, recv2b, sum3, recv3,
-    load_sem, d_sem, t_sem, s0, r0, s1a, r1a, s1b, r1b, s2a, r2a, s2b, r2b, s3, r3,
+    load_sem, d_sem, t_sem, relay, s0, r0, s1a, r1a, s1b, r1b, s2a, r2a, s2b, r2b, s3, r3,
 ):
     yn, zn, slots, share, width = dims
     half = width // 2
@@ -44,10 +44,14 @@
     y_ids = [lax.rem(y + d, yn) for d in range(1, yn)]
     y_peers = [dev(i, c, z, x) for i in y_ids]
     z_peers = [dev(y, c, lax.rem(z + d, zn), x) for d in shifts]
-    peers = [core_peer, x_peer] + y_peers + z_peers
+    z_near = [dev(y, c, lax.rem(z + d, zn), x) for d in {1 % zn, (zn - 1) % zn} - {0}]
+    near = [core_peer, x_peer] + y_peers + z_near
+    prev_z = dev(y, c, lax.rem(z + zn - 1, zn), x)
 
     t_load = pltpu.make_async_copy(targets_in, targets, t_sem)
     t_load.start()
+    d_load = pltpu.make_async_copy(diag.at[0], dbuf, d_sem)
+    d_load.start()
     loads = []
     for s in range(slots):
         pair = (
@@ -57,38 +61,78 @@
         for copy in pair:
             copy.start()
         loads.append(pair)
-    d_load = pltpu.make_async_copy(diag.at[0], dbuf, d_sem)
-    d_load.start()
 
     barrier = pltpu.get_barrier_semaphore()
-    for peer in peers:
+    for peer in near:
         pl.semaphore_signal(barrier, inc=1, device_id=peer, device_id_type=MESH)
 
-    for s in range(slots):
-        for copy in loads[s]:
-            copy.wait()
-        prod[s] = gram_dot(lbuf[s], abuf[s]).reshape(yn, 2, share, width)
+    t_load.wait()
+    ids = [targets[0, s] for s in range(slots)] + [col]
+    count = len(ids)
+
+    def less(k):
+        total = jnp.int32(0)
+        for t in ids:
+            total = total + (t < k).astype(jnp.int32)
+        return total
+
+    ranks = []
+    for s in range(count):
+        rank = jnp.int32(0)
+        for r in range(count):
+            ahead = ids[r] <= ids[s] if r < s else ids[r] < ids[s]
+            if r != s:
+                rank = rank + ahead.astype(jnp.int32)
+        ranks.append(rank)
+    sorted_slots = []
+    for j in range(count):
+        slot = jnp.int32(0)
+        for s in range(1, count):
+            slot = slot + jnp.where(ranks[s] == j, s, 0)
+        sorted_slots.append(slot)
+
     d_load.wait()
-    t_load.wait()
-    prod[slots] = gram_dot(dbuf[...], dbuf[...]).reshape(yn, 2, share, width)
-
-    def segment(o, side, dest):
-        zd = lax.rem(z + order[o], zn)
+    prod[slots] = -gram_dot(dbuf[...], dbuf[...]).reshape(yn, 2, share, width)
+    first = 0
+    for group in (1, slots - 1):
+        for s in range(first, first + group):
+            for copy in loads[s]:
+                copy.wait()
+        for s in range(first, first + group):
+            prod[s] = gram_dot(lbuf[s], abuf[s]).reshape(yn, 2, share, width)
+        first += group
+
+    def prefix(side):
+        for yo in range(yn):
+            cum[0, yo, side] = jnp.zeros((share, width), jnp.float32)
+            total = prod[sorted_slots[0], yo, side]
+            cum[1, yo, side] = total
+            for j in range(1, count):
+                total = total + prod[sorted_slots[j], yo, side]
+                cum[j + 1, yo, side] = total
+
+    bounds = {}
+    for o in range(zn):
         for xi in range(2):
-            k = zd * 2 + xi
-            weights = [jnp.where(targets[0, s] == k, -1.0, 0.0) for s in range(slots)]
-            weights.append(jnp.where(col == k, 1.0, 0.0))
-
-            def body(yo, carry):
+            k = lax.rem(z + order[o], zn) * 2 + xi
+            bounds[o, xi] = (less(k), less(k + 1))
+
+    def part(o, h, xi, yo, side):
+        lanes = slice(h * half, (h + 1) * half)
+        begin, end = bounds[o, xi]
+        return cum[begin, yo, side, :, lanes] - cum[end, yo, side, :, lanes]
+
+    def dynamic_part(o, h, xi, yo):
+        lanes = slice(h * half, (h + 1) * half)
+        begin = jnp.where(xi == 0, bounds[o, 0][0], bounds[o, 1][0])
+        end = jnp.where(xi == 0, bounds[o, 0][1], bounds[o, 1][1])
+        return cum[begin, yo, c, :, lanes] - cum[end, yo, c, :, lanes]
+
+    def segment(o):
+        for xi in range(2):
+            for yo in range(yn):
                 for h in range(2):
-                    lanes = slice(h * half, (h + 1) * half)
-                    total = weights[0] * prod[0, yo, side, :, lanes]
-                    for s in range(1, slots + 1):
-                        total = total + weights[s] * prod[s, yo, side, :, lanes]
-                    dest[o, h, xi, yo] = total
-                return carry
-
-            lax.fori_loop(0, yn, body, 0)
+                    send0[o, h, xi, yo] = part(o, h, xi, yo, 1 - c)
 
     def remote(src, dst, send, recv, peer):
         copy = pltpu.make_async_remote_copy(
@@ -107,10 +151,11 @@
 
     def stage1(o):
         copies0[o].wait_recv()
-        send1a[o] = own0[o, 0, 1 - x] + recv0[o, 0, 1 - x]
+        for yo in range(yn):
+            send1a[o, yo] = dynamic_part(o, 0, 1 - x, yo) + recv0[o, 0, 1 - x, yo]
         for i, yo in enumerate(y_ids):
             for xi in range(2):
-                send1b[o, i, xi] = own0[o, 1, xi, yo] + recv0[o, 1, xi, yo]
+                send1b[o, i, xi] = part(o, 1, xi, yo, c) + recv0[o, 1, xi, yo]
         copies1a[o] = remote(send1a.at[o], recv1a.at[o], s1a.at[o], r1a.at[o], x_peer)
         copies1b[o] = [
             remote(send1b.at[o, i], recv1b.at[o, i], s1b.at[o, i], r1b.at[o, i], peer)
@@ -120,7 +165,8 @@
 
     def stage2(o):
         copies1a[o].wait_recv()
-        sum2a[o] = own0[o, 0, x] + recv0[o, 0, x] + recv1a[o]
+        for yo in range(yn):
+            sum2a[o, yo] = dynamic_part(o, 0, x, yo) + recv0[o, 0, x, yo] + recv1a[o, yo]
         copies2a[o] = [
             remote(sum2a.at[o, yo], recv2a.at[o, i], s2a.at[o, i], r2a.at[o, i], peer)
             for i, (yo, peer) in enumerate(zip(y_ids, y_peers))
@@ -128,7 +174,7 @@
         for copy in copies1b[o]:
             copy.wait_recv()
         for xi in range(2):
-            total = own0[o, 1, xi, y] + recv0[o, 1, xi, y]
+            total = part(o, 1, xi, y, c) + recv0[o, 1, xi, y]
             for i in range(yn - 1):
                 total = total + recv1b[o, i, xi]
             sum2b[o, xi] = total
@@ -151,16 +197,21 @@
             copies3[o] = (first, second)
             started.extend(copies3[o])
 
+    prefix(1 - c)
     for o in range(zn):
-        segment(o, 1 - c, send0)
+        segment(o)
         if o == 0:
-            pl.semaphore_wait(barrier, len(peers))
+            pl.semaphore_wait(barrier, len(near))
         stage0(o)
+    if zn > 2:
+        pl.semaphore_signal(relay, inc=1, device_id=prev_z, device_id_type=MESH)
+    prefix(c)
     ahead, lag = 2, 2
     for step in range(zn + ahead + lag):
         if step < zn:
-            segment(step, c, own0)
             stage1(step)
+        if step == ahead + lag and zn > 2:
+            pl.semaphore_wait(relay, 1)
         if 0 <= step - ahead < zn:
             stage2(step - ahead)
         if 0 <= step - ahead - lag < zn:
@@ -191,7 +242,7 @@
         pltpu.VMEM((slots, height, width), f32),
         pltpu.VMEM((share, width), f32),
         pltpu.VMEM((slots + 1, yn, 2, share, width), f32),
-        pltpu.VMEM((zn, 2, 2, yn) + tail, f32),
+        pltpu.VMEM((slots + 2, yn, 2, share, width), f32),
         pltpu.VMEM((zn, 2, 2, yn) + tail, f32),
         pltpu.VMEM((zn, 2, 2, yn) + tail, f32),
         pltpu.VMEM((zn, yn) + tail, f32),
@@ -204,7 +255,7 @@
         pltpu.VMEM((zn,) + tail, f32),
         pltpu.VMEM((zn, 2) + tail, f32),
         pltpu.VMEM((zn - 1, 2) + tail, f32),
-        dma((slots, 2)), dma, dma,
+        dma((slots, 2)), dma, dma, pltpu.SemaphoreType.REGULAR,
         dma((zn,)), dma((zn,)),
         dma((zn,)), dma((zn,)),
         dma((zn, yn - 1)), dma((zn, yn - 1)),

time: 24.8 us -> 24.2 us (0.976)
  Pallas kernels: 24 us -> 23.4 us
    pallas_call x1, Pallas kernels: 24 us -> 23.4 us  [on_device(): pl.pallas_call(functools.partial(kernel, (yn, zn, slots, share, width)),...]
where the time goes in v1:
time: 24.2 us; the launch traced here: 24 us
  Pallas kernels  23.4 us (97%)
  local copies, waits for them, and re-layouts  0.63 us (3%)
    pallas_call x1, Pallas kernels, on_device(): pl.pallas_call(functools.partial(kernel, (yn, zn, slots, share, width)),...  23.4 us
    unnamed x1, local copies, waits for them, and re-layouts  0.63 us

profile of v1, /device:TPU:0, one launch (start us, length us, event | category | flops | bytes accessed | tf_op | source)
XLA Modules:
  0.0 24.0 jit_solution(7787908702304589460)
XLA Ops:
  0.0 23.4 %shard_map.46 = f32[1,64,256]{2,1,0:T(8,128)S(1)} custom-call(f32[8,256,256]{2,1,0:T(8,128)} %lhat.1, f32[8,256,256]{2,1,0:T(8,128)} %ainv.1, f32[1,64,256]{2,1,0:T(8,128)} %diag.1, s32[1,8]{1,0:T(1,128)} %bitcast.1), custom_call_target="tpu_custom_call" | custom-call | tf_op jit(solution)/shard_map/pallas_call | solution.py:266
  23.4 0.6 %copy.6 = f32[1,64,256]{2,1,0:T(8,128)} copy(f32[1,64,256]{2,1,0:T(8,128)S(1)} %shard_map.46) | data formatting | bytes 131072

commit v2 on v1

--- a/solution.py
+++ b/solution.py
@@ -37,13 +37,13 @@
     def dev(y_, c_, z_, x_):
         return {"row": y_ * 2 + c_, "col": z_ * 2 + x_}
 
-    shifts = [zn // 2] + [d for d in range(1, zn) if d != zn // 2] if zn > 1 else []
-    order = shifts + [0]
+    order = [jnp.where(o < z, o, o + 1) for o in range(zn - 1)] + [z]
     core_peer = dev(y, 1 - c, z, x)
     x_peer = dev(y, c, z, 1 - x)
     y_ids = [lax.rem(y + d, yn) for d in range(1, yn)]
     y_peers = [dev(i, c, z, x) for i in y_ids]
-    z_peers = [dev(y, c, lax.rem(z + d, zn), x) for d in shifts]
+    z_peers = [dev(y, c, zd, x) for zd in order[:-1]]
+    z_slots = [jnp.where(z < zd, z, z - 1) for zd in order[:-1]]
     z_near = [dev(y, c, lax.rem(z + d, zn), x) for d in {1 % zn, (zn - 1) % zn} - {0}]
     near = [core_peer, x_peer] + y_peers + z_near
     prev_z = dev(y, c, lax.rem(z + zn - 1, zn), x)
@@ -66,6 +66,13 @@
     for peer in near:
         pl.semaphore_signal(barrier, inc=1, device_id=peer, device_id_type=MESH)
 
+    for copy in loads[0]:
+        copy.wait()
+    prod[0] = gram_dot(lbuf[0], abuf[0]).reshape(yn, 2, share, width)
+    for s in range(1, slots):
+        for copy in loads[s]:
+            copy.wait()
+    d_load.wait()
     t_load.wait()
     ids = [targets[0, s] for s in range(slots)] + [col]
     count = len(ids)
@@ -91,16 +98,9 @@
             slot = slot + jnp.where(ranks[s] == j, s, 0)
         sorted_slots.append(slot)
 
-    d_load.wait()
+    for s in range(1, slots):
+        prod[s] = gram_dot(lbuf[s], abuf[s]).reshape(yn, 2, share, width)
     prod[slots] = -gram_dot(dbuf[...], dbuf[...]).reshape(yn, 2, share, width)
-    first = 0
-    for group in (1, slots - 1):
-        for s in range(first, first + group):
-            for copy in loads[s]:
-                copy.wait()
-        for s in range(first, first + group):
-            prod[s] = gram_dot(lbuf[s], abuf[s]).reshape(yn, 2, share, width)
-        first += group
 
     def prefix(side):
         for yo in range(yn):
@@ -114,7 +114,7 @@
     bounds = {}
     for o in range(zn):
         for xi in range(2):
-            k = lax.rem(z + order[o], zn) * 2 + xi
+            k = order[o] * 2 + xi
             bounds[o, xi] = (less(k), less(k + 1))
 
     def part(o, h, xi, yo, side):
@@ -189,11 +189,11 @@
             total = total + recv2a[o, i]
         sum3[o, 0] = total
         if o < zn - 1:
-            first = remote(sum3.at[o, 0], recv3.at[o, 0], s3.at[o, 0], r3.at[o, 0], z_peers[o])
+            first = remote(sum3.at[o, 0], recv3.at[z_slots[o], 0], s3.at[o, 0], r3.at[z_slots[o], 0], z_peers[o])
         copies2b[o].wait_recv()
         sum3[o, 1] = sum2b[o, x] + recv2b[o]
         if o < zn - 1:
-            second = remote(sum3.at[o, 1], recv3.at[o, 1], s3.at[o, 1], r3.at[o, 1], z_peers[o])
+            second = remote(sum3.at[o, 1], recv3.at[z_slots[o], 1], s3.at[o, 1], r3.at[z_slots[o], 1], z_peers[o])
             copies3[o] = (first, second)
             started.extend(copies3[o])
 
@@ -217,10 +217,16 @@
         if 0 <= step - ahead - lag < zn:
             stage3(step - ahead - lag)
 
+    def incoming(i, h):
+        return pltpu.make_async_remote_copy(
+            src_ref=recv3.at[i, h], dst_ref=recv3.at[i, h], send_sem=s3.at[i, h], recv_sem=r3.at[i, h],
+            device_id=core_peer, device_id_type=MESH,
+        )
+
     totals = [sum3[zn - 1, h] for h in range(2)]
     for o in range(zn - 1):
         for h in range(2):
-            copies3[o][h].wait_recv()
+            incoming(o, h).wait_recv()
             totals[h] = totals[h] + recv3[o, h]
     for h in range(2):
         out[0, :, h * half:(h + 1) * half] = totals[h]

time: 24.2 us -> 22.6 us (0.934)
  Pallas kernels: 23.4 us -> 21.8 us
    pallas_call x1, Pallas kernels: 23.4 us -> 21.8 us  [on_device(): pl.pallas_call(functools.partial(kernel, (yn, zn, slots, share, width)),...]
where the time goes in v2:
time: 22.6 us; the launch traced here: 22.4 us
  Pallas kernels  21.8 us (96%)
  local copies, waits for them, and re-layouts  0.63 us (3%)
    pallas_call x1, Pallas kernels, on_device(): pl.pallas_call(functools.partial(kernel, (yn, zn, slots, share, width)),...  21.8 us
    unnamed x1, local copies, waits for them, and re-layouts  0.63 us

profile of v2, /device:TPU:0, one launch (start us, length us, event | category | flops | bytes accessed | tf_op | source)
XLA Modules:
  0.0 22.4 jit_solution(3380905905708415654)
XLA Ops:
  0.0 21.8 %shard_map.46 = f32[1,64,256]{2,1,0:T(8,128)S(1)} custom-call(f32[8,256,256]{2,1,0:T(8,128)} %lhat.1, f32[8,256,256]{2,1,0:T(8,128)} %ainv.1, f32[1,64,256]{2,1,0:T(8,128)} %diag.1, s32[1,8]{1,0:T(1,128)} %bitcast.1), custom_call_target="tpu_custom_call" | custom-call | tf_op jit(solution)/shard_map/pallas_call | solution.py:272
  21.8 0.6 %copy.6 = f32[1,64,256]{2,1,0:T(8,128)} copy(f32[1,64,256]{2,1,0:T(8,128)S(1)} %shard_map.46) | data formatting | bytes 131072

commit v3 on v2

v3 whole, which is shorter than its diff:
```python
import functools

import jax
import jax.numpy as jnp
from jax import lax
from jax.experimental import pallas as pl
from jax.experimental.pallas import tpu as pltpu
from jax.sharding import PartitionSpec as P

MESH = pl.DeviceIdType.MESH
DN = (((0,), (0,)), ((), ()))


def gram_dot(a, b):
    a_hi = a.astype(jnp.bfloat16)
    a_lo = (a - a_hi.astype(jnp.float32)).astype(jnp.bfloat16)
    b_hi = b.astype(jnp.bfloat16)
    b_lo = (b - b_hi.astype(jnp.float32)).astype(jnp.bfloat16)
    left = jnp.concatenate([a_hi, a_lo, a_hi], axis=0)
    right = jnp.concatenate([b_hi, b_hi, b_lo], axis=0)
    return lax.dot_general(left, right, DN, preferred_element_type=jnp.float32)


def top_rows(share):
    return share // 4 // 8 * 8


def kernel(
    dims,
    lhat, ainv, diag, targets_in, out,
    targets, lbuf, abuf, dbuf, prod, cum,
    send0, recv0, send1, recv1, sum2a, sum2b, recv2, sum3, recv3,
    tsend0, trecv0, tsend1, trecv1, tsum, trecv2,
    load_sem, relay, s0, r0, s1, r1, s2, r2, s3, r3, top_sem,
):
    yn, zn, slots, share, width = dims
    half = width // 2
    top = top_rows(share)
    row, col = lax.axis_index("row"), lax.axis_index("col")
    y, c = lax.div(row, 2), lax.rem(row, 2)
    z, x = lax.div(col, 2), lax.rem(col, 2)

    def dev(y_, c_, z_, x_):
        return {"row": y_ * 2 + c_, "col": z_ * 2 + x_}

    order = [jnp.where(o < z, o, o + 1) for o in range(zn - 1)] + [z]
    core_peer = dev(y, 1 - c, z, x)
    x_peer = dev(y, c, z, 1 - x)
    y_ids = [lax.rem(y + d, yn) for d in range(1, yn)]
    y_peers = [dev(i, c, z, x) for i in y_ids]
    z_peers = [dev(y, c, zd, x) for zd in order[:-1]]
    z_slots = [jnp.where(z < zd, z, z - 1) for zd in order[:-1]]
    shifts = sorted(range(1, zn), key=lambda d: min(d, zn - d))
    ring = [dev(y, c, lax.rem(z + d, zn), x) for d in (1, zn - 1)]
    near = [core_peer, x_peer] + y_peers + ring

    def local(src, dst, sem):
        return pltpu.make_async_copy(src, dst, sem)

    t_load = local(targets_in, targets, load_sem.at[0])
    t_load.start()
    d_load = local(diag.at[0], dbuf, load_sem.at[1])
    d_load.start()
    for s in range(slots):
        first = s == 0
        local(lhat.at[s], lbuf.at[s], load_sem.at[2 if first else 3]).start()
        local(ainv.at[s], abuf.at[s], load_sem.at[2 if first else 4]).start()

    barrier = pltpu.get_barrier_semaphore()
    for peer in near:
        pl.semaphore_signal(barrier, inc=1, device_id=peer, device_id_type=MESH)

    pair = lbuf.at[pl.ds(0, 2)]
    local(pair, pair, load_sem.at[2]).wait()
    prod[0] = gram_dot(lbuf[0], abuf[0]).reshape(yn, 2, share, width)
    rest = pl.ds(1, slots - 1)
    local(lhat.at[rest], lbuf.at[rest], load_sem.at[3]).wait()
    local(ainv.at[rest], abuf.at[rest], load_sem.at[4]).wait()
    d_load.wait()
    t_load.wait()

    ids = [targets[0, s] for s in range(slots)] + [col]
    count = len(ids)

    def less(k):
        total = jnp.int32(0)
        for t in ids:
            total = total + (t < k).astype(jnp.int32)
        return total

    ranks = []
    for s in range(count):
        rank = jnp.int32(0)
        for r in range(count):
            if r != s:
                before = ids[r] <= ids[s] if r < s else ids[r] < ids[s]
                rank = rank + before.astype(jnp.int32)
        ranks.append(rank)
    sorted_slots = []
    for j in range(count):
        slot = jnp.int32(0)
        for s in range(1, count):
            slot = slot + jnp.where(ranks[s] == j, s, 0)
        sorted_slots.append(slot)

    for s in range(1, slots):
        prod[s] = gram_dot(lbuf[s], abuf[s]).reshape(yn, 2, share, width)
    prod[slots] = -gram_dot(dbuf[...], dbuf[...]).reshape(yn, 2, share, width)

    def prefix(side):
        for yo in range(yn):
            cum[0, yo, side] = jnp.zeros((share, width), jnp.float32)
            total = prod[sorted_slots[0], yo, side]
            cum[1, yo, side] = total
            for j in range(1, count):
                total = total + prod[sorted_slots[j], yo, side]
                cum[j + 1, yo, side] = total

    bounds = {}
    for o in range(zn):
        for xi in range(2):
            k = order[o] * 2 + xi
            bounds[o, xi] = (less(k), less(k + 1))
    top_bounds = {}
    for i, d in enumerate(shifts + [0]):
        for xi in range(2):
            k = lax.rem(z + d, zn) * 2 + xi
            top_bounds[i, xi] = (less(k), less(k + 1))

    def lanes(h):
        return slice(h * half, (h + 1) * half)

    def part(o, h, xi, yo, side):
        begin, end = bounds[o, xi]
        return cum[begin, yo, side, top:, lanes(h)] - cum[end, yo, side, top:, lanes(h)]

    def own_part(o, xi, yo):
        begin = jnp.where(xi == 0, bounds[o, 0][0], bounds[o, 1][0])
        end = jnp.where(xi == 0, bounds[o, 0][1], bounds[o, 1][1])
        return cum[begin, yo, c, top:, lanes(0)] - cum[end, yo, c, top:, lanes(0)]

    def top_part(i, xi, yo, side):
        begin, end = top_bounds[i, xi]
        return cum[begin, yo, side, :top] - cum[end, yo, side, :top]

    def remote(src, dst, send, recv, peer):
        copy = pltpu.make_async_remote_copy(
            src_ref=src, dst_ref=dst, send_sem=send, recv_sem=recv, device_id=peer, device_id_type=MESH
        )
        copy.start()

    def settle(ref, sem):
        local(ref, ref, sem).wait()

    def stage0(o):
        for xi in range(2):
            for yo in range(yn):
                for h in range(2):
                    send0[o, h, xi, yo] = part(o, h, xi, yo, 1 - c)
        if o == 0:
            pl.semaphore_wait(barrier, len(near))
        remote(send0.at[o], recv0.at[o], s0, r0.at[o], core_peer)

    def stage1(o):
        settle(recv0.at[o], r0.at[o])
        for yo in range(yn):
            send1[o, yo] = own_part(o, 1 - x, yo) + recv0[o, 0, 1 - x, yo]
        block = pl.ds(0, yn)
        remote(send1.at[o, block], recv1.at[o, block], s1, r1.at[o], x_peer)
        for i, yo in enumerate(y_ids):
            for xi in range(2):
                send1[o, yn + 2 * i + xi] = part(o, 1, xi, yo, c) + recv0[o, 1, xi, yo]
            block = pl.ds(yn + 2 * i, 2)
            remote(send1.at[o, block], recv1.at[o, block], s1, r1.at[o], y_peers[i])

    def stage2(o):
        settle(recv1.at[o], r1.at[o])
        for yo in range(yn):
            sum2a[o, yo] = own_part(o, x, yo) + recv0[o, 0, x, yo] + recv1[o, yo]
        for i, yo in enumerate(y_ids):
            remote(sum2a.at[o, yo], recv2.at[o, i], s2, r2.at[o], y_peers[i])
        for xi in range(2):
            total = part(o, 1, xi, y, c) + recv0[o, 1, xi, y]
            for i in range(yn - 1):
                total = total + recv1[o, yn + 2 * i + xi]
            sum2b[o, xi] = total
        remote(sum2b.at[o, 1 - x], recv2.at[o, yn - 1], s2, r2.at[o], x_peer)

    def stage3(o):
        settle(recv2.at[o], r2.at[o])
        total = sum2a[o, y]
        for i in range(yn - 1):
            total = total + recv2[o, i]
        sum3[o, 0] = total
        sum3[o, 1] = sum2b[o, x] + recv2[o, yn - 1]
        if o < zn - 1:
            remote(sum3.at[o], recv3.at[z_slots[o]], s3, r3, z_peers[o])

    def top_stage0():
        for i in range(zn):
            for xi in range(2):
                for yo in range(yn):
                    tsend0[i, xi, yo] = top_part(i, xi, yo, 1 - c)
        remote(tsend0, trecv0, top_sem.at[0], top_sem.at[1], core_peer)

    def top_stage1(i):
        for xi in range(2):
            for yo in range(yn):
                tsend1[i, xi, yo] = top_part(i, xi, yo, c) + trecv0[i, xi, yo]
        peer = dev(y, c, lax.rem(z + shifts[i], zn), x)
        remote(tsend1.at[i], trecv1.at[i], top_sem.at[2], top_sem.at[3], peer)

    def top_stage2():
        settle(trecv1, top_sem.at[3])
        for xi in range(2):
            for yo in range(yn):
                total = top_part(zn - 1, xi, yo, c) + trecv0[zn - 1, xi, yo]
                for i in range(zn - 1):
                    total = total + trecv1[i, xi, yo]
                tsum[xi, yo] = total
        for dx in range(2):
            for dy in range(yn):
                if dx or dy:
                    xo, yo = lax.rem(x + dx, 2), lax.rem(y + dy, yn)
                    i = dx * yn + dy - 1
                    remote(tsum.at[xo, yo], trecv2.at[i], top_sem.at[4], top_sem.at[5], dev(yo, c, z, xo))

    def greet(r):
        for peer in ring:
            pl.semaphore_signal(relay.at[r], inc=1, device_id=peer, device_id_type=MESH)

    hops = zn // 2 - 1
    prefix(1 - c)
    stage0(0)
    if hops:
        greet(0)
    if top:
        top_stage0()
    for o in range(1, zn):
        stage0(o)
    prefix(c)
    stage1(0)
    if top:
        settle(trecv0, top_sem.at[1])
        for i in range(2):
            top_stage1(i)
    for o in range(1, zn):
        stage1(o)
    for r in range(hops):
        pl.semaphore_wait(relay.at[r], 2)
        if r < hops - 1:
            greet(r + 1)
    if top:
        for i in range(2, zn - 1):
            top_stage1(i)
    for o in range(zn):
        stage2(o)
    stage3(0)
    if top:
        top_stage2()
    for o in range(1, zn):
        stage3(o)

    settle(recv3, r3)
    for h in range(2):
        total = sum3[zn - 1, h]
        for i in range(zn - 1):
            total = total + recv3[i, h]
        out[0, top:, lanes(h)] = total
    if top:
        settle(trecv2, top_sem.at[5])
        total = tsum[x, y]
        for i in range(2 * yn - 1):
            total = total + trecv2[i]
        out[0, :top] = total
        settle(tsend0, top_sem.at[0])
        settle(tsend1, top_sem.at[2])
        settle(trecv2, top_sem.at[4])
    settle(send0, s0)
    settle(send1, s1)
    settle(recv2, s2)
    settle(recv3, s3)


def on_device(lhat, ainv, diag, targets):
    rows, cols = lax.axis_size("row"), lax.axis_size("col")
    slots, width = lhat.shape[0], lhat.shape[2]
    height = lhat.shape[1]
    yn, zn, share = rows // 2, cols // 2, diag.shape[1]
    half = width // 2
    f32, dma = jnp.float32, pltpu.SemaphoreType.DMA
    top = top_rows(share)
    low = (share - top, half)
    high = (max(top, 8), width)
    scratch = [
        pltpu.SMEM((1, slots), jnp.int32),
        pltpu.VMEM((slots, height, width), f32),
        pltpu.VMEM((slots, height, width), f32),
        pltpu.VMEM((share, width), f32),
        pltpu.VMEM((slots + 1, yn, 2, share, width), f32),
        pltpu.VMEM((slots + 2, yn, 2, share, width), f32),
        pltpu.VMEM((zn, 2, 2, yn) + low, f32),
        pltpu.VMEM((zn, 2, 2, yn) + low, f32),
        pltpu.VMEM((zn, 3 * yn - 2) + low, f32),
        pltpu.VMEM((zn, 3 * yn - 2) + low, f32),
        pltpu.VMEM((zn, yn) + low, f32),
        pltpu.VMEM((zn, 2) + low, f32),
        pltpu.VMEM((zn, yn) + low, f32),
        pltpu.VMEM((zn, 2) + low, f32),
        pltpu.VMEM((zn - 1, 2) + low, f32),
        pltpu.VMEM((zn, 2, yn) + high, f32),
        pltpu.VMEM((zn, 2, yn) + high, f32),
        pltpu.VMEM((zn - 1, 2, yn) + high, f32),
        pltpu.VMEM((zn - 1, 2, yn) + high, f32),
        pltpu.VMEM((2, yn) + high, f32),
        pltpu.VMEM((2 * yn - 1,) + high, f32),
        dma((5,)), pltpu.SemaphoreType.REGULAR((max(zn // 2 - 1, 1),)),
        dma, dma((zn,)), dma, dma((zn,)), dma, dma((zn,)), dma, dma, dma((6,)),
    ]
    return pl.pallas_call(
        functools.partial(kernel, (yn, zn, slots, share, width)),
        out_shape=pltpu.VMEM(diag.shape, f32),
        in_specs=[pl.BlockSpec(memory_space=pltpu.HBM)] * 4,
        out_specs=pl.BlockSpec(memory_space=pltpu.VMEM),
        scratch_shapes=scratch,
        compiler_params=pltpu.CompilerParams(
            collective_id=0, has_side_effects=True, vmem_limit_bytes=60 * 1024 * 1024
        ),
    )(lhat, ainv, diag, targets.T)


def solution(mesh):
    placed = (
        P(("row", "col"), None, None),
        P(("row", "col"), None, None),
        P("col", "row", None),
        P(("row", "col"), None),
    )
    return jax.shard_map(
        on_device, mesh=mesh, in_specs=placed, out_specs=P("col", "row", None), check_vma=False
    )
```

time: 22.6 us -> 21.7 us (0.960)
  Pallas kernels: 21.8 us -> 20.9 us
    pallas_call x1, Pallas kernels: 21.8 us -> 20.9 us  [on_device(): pl.pallas_call(functools.partial(kernel, (yn, zn, slots, share, width)),...]
where the time goes in v3:
time: 21.7 us; the launch traced here: 21.6 us
  Pallas kernels  20.9 us (96%)
  local copies, waits for them, and re-layouts  0.63 us (3%)
    pallas_call x1, Pallas kernels, on_device(): pl.pallas_call(functools.partial(kernel, (yn, zn, slots, share, width)),...  20.9 us
    unnamed x1, local copies, waits for them, and re-layouts  0.63 us

profile of v3, /device:TPU:0, one launch (start us, length us, event | category | flops | bytes accessed | tf_op | source)
XLA Modules:
  0.0 21.6 jit_solution(14767712188460993169)
XLA Ops:
  0.0 20.9 %shard_map.46 = f32[1,64,256]{2,1,0:T(8,128)S(1)} custom-call(f32[8,256,256]{2,1,0:T(8,128)} %lhat.1, f32[8,256,256]{2,1,0:T(8,128)} %ainv.1, f32[1,64,256]{2,1,0:T(8,128)} %diag.1, s32[1,8]{1,0:T(1,128)} %bitcast.1), custom_call_target="tpu_custom_call" | custom-call | tf_op jit(solution)/shard_map/pallas_call | solution.py:320
  20.9 0.6 %copy.6 = f32[1,64,256]{2,1,0:T(8,128)} copy(f32[1,64,256]{2,1,0:T(8,128)S(1)} %shard_map.46) | data formatting | bytes 131072

commit v4 on v3

v4 whole, which is shorter than its diff:
```python
import functools

import jax
import jax.numpy as jnp
from jax import lax
from jax.experimental import pallas as pl
from jax.experimental.pallas import tpu as pltpu
from jax.sharding import PartitionSpec as P

MESH = pl.DeviceIdType.MESH
DN = (((0,), (0,)), ((), ()))
HOLD = 1
T2 = 6


def gram_dot(a, b):
    a_hi = a.astype(jnp.bfloat16)
    a_lo = (a - a_hi.astype(jnp.float32)).astype(jnp.bfloat16)
    b_hi = b.astype(jnp.bfloat16)
    b_lo = (b - b_hi.astype(jnp.float32)).astype(jnp.bfloat16)
    left = jnp.concatenate([a_hi, a_lo, a_hi], axis=0)
    right = jnp.concatenate([b_hi, b_hi, b_lo], axis=0)
    return lax.dot_general(left, right, DN, preferred_element_type=jnp.float32)


def kernel(
    dims,
    lhat, ainv, diag, targets_in, out,
    targets, lbuf, abuf, dbuf, prod, cum,
    send0, recv0, send1, recv1, sum2a, sum2b, recv2, frecv2, sum3, recv3,
    tsend0, trecv0, tsend1, trecv1, tsum, trecv2,
    load_sem, relay, s0, r0, s1, r1, s2, r2, fs2, fr2, s3, r3, top_sem,
):
    yn, zn, slots, share, width = dims
    half = width // 2
    rows = share // 2
    row, col = lax.axis_index("row"), lax.axis_index("col")
    y, c = lax.div(row, 2), lax.rem(row, 2)
    z, x = lax.div(col, 2), lax.rem(col, 2)

    def dev(y_, c_, z_, x_):
        return {"row": y_ * 2 + c_, "col": z_ * 2 + x_}

    def by_plane(values):
        total = jnp.int32(0)
        for q in range(zn):
            total = total + jnp.where(z == q, values[q], 0)
        return total

    far = [[d for d in [0] + list(range(zn - 1, 0, -1)) if d // 2 != q // 2] for q in range(zn)]
    order = [by_plane([far[q][o] for q in range(zn)]) for o in range(zn - 2)] + [z + 1 - 2 * lax.rem(z, 2), z]
    seat = [by_plane([[d for d in far[q] if d % 2 == far[q][o] % 2].index(far[q][o]) for q in range(zn)]) for o in range(zn - 2)]
    kept = zn // 2 - 1
    mine = [[[o for o, d in enumerate(far[q]) if d % 2 == q % 2][e] for q in range(zn)] for e in range(kept)]
    place = [by_plane(mine[e]) for e in range(kept)]
    goal = [by_plane([far[q][mine[e][q]] for q in range(zn)]) for e in range(kept)]
    chunks = [(o, h) for o in range(zn - 2) for h in range(2)] + [(zn - 2, 1), (zn - 1, 1)]
    n_far = 2 * (zn - 2)
    core_peer = dev(y, 1 - c, z, x)
    x_peer = dev(y, c, z, 1 - x)
    y_ids = [lax.rem(y + d, yn) for d in range(1, yn)]
    y_peers = [dev(i, c, z, x) for i in y_ids]
    mate = dev(y, c, z + 1 - 2 * lax.rem(z, 2), x)
    below, above = z > 0, z < zn - 1
    line = [(below, dev(y, c, z - 1, x)), (above, dev(y, c, z + 1, x))]
    n_line = below.astype(jnp.int32) + above.astype(jnp.int32)
    near = [core_peer, x_peer] + y_peers

    def greet(sem):
        for there, peer in line:

            @pl.when(there)
            def _():
                pl.semaphore_signal(sem, inc=1, device_id=peer, device_id_type=MESH)

    def local(src, dst, sem):
        return pltpu.make_async_copy(src, dst, sem)

    t_load = local(targets_in, targets, load_sem.at[0])
    t_load.start()
    d_load = local(diag.at[0], dbuf, load_sem.at[1])
    d_load.start()
    for s in range(slots):
        first = s == 0
        local(lhat.at[s], lbuf.at[s], load_sem.at[2 if first else 3]).start()
        local(ainv.at[s], abuf.at[s], load_sem.at[2 if first else 4]).start()

    barrier = pltpu.get_barrier_semaphore()
    for peer in near:
        pl.semaphore_signal(barrier, inc=1, device_id=peer, device_id_type=MESH)
    greet(barrier)

    pair = lbuf.at[pl.ds(0, 2)]
    local(pair, pair, load_sem.at[2]).wait()
    prod[0] = gram_dot(lbuf[0], abuf[0]).reshape(yn, 2, share, width)
    rest = pl.ds(1, slots - 1)
    local(lhat.at[rest], lbuf.at[rest], load_sem.at[3]).wait()
    local(ainv.at[rest], abuf.at[rest], load_sem.at[4]).wait()
    d_load.wait()
    t_load.wait()

    ids = [targets[0, s] for s in range(slots)] + [col]
    count = len(ids)

    def less(k):
        total = jnp.int32(0)
        for t in ids:
            total = total + (t < k).astype(jnp.int32)
        return total

    ranks = []
    for s in range(count):
        rank = jnp.int32(0)
        for r in range(count):
            if r != s:
                before = ids[r] <= ids[s] if r < s else ids[r] < ids[s]
                rank = rank + before.astype(jnp.int32)
        ranks.append(rank)
    sorted_slots = []
    for j in range(count):
        slot = jnp.int32(0)
        for s in range(1, count):
            slot = slot + jnp.where(ranks[s] == j, s, 0)
        sorted_slots.append(slot)

    for s in range(1, slots):
        prod[s] = gram_dot(lbuf[s], abuf[s]).reshape(yn, 2, share, width)
    prod[slots] = -gram_dot(dbuf[...], dbuf[...]).reshape(yn, 2, share, width)

    def prefix(side):
        for yo in range(yn):
            cum[0, yo, side] = jnp.zeros((share, width), jnp.float32)
            total = prod[sorted_slots[0], yo, side]
            cum[1, yo, side] = total
            for j in range(1, count):
                total = total + prod[sorted_slots[j], yo, side]
                cum[j + 1, yo, side] = total

    bounds = {}
    for o in range(zn):
        for xi in range(2):
            k = order[o] * 2 + xi
            bounds[o, xi] = (less(k), less(k + 1))

    def lanes(h):
        return slice(h * half, (h + 1) * half)

    def span(h):
        return slice(h * rows, (h + 1) * rows)

    def part(i, h, xi, yo, side):
        o, upper = chunks[i]
        begin, end = bounds[o, xi]
        return cum[begin, yo, side, span(upper), lanes(h)] - cum[end, yo, side, span(upper), lanes(h)]

    def own_part(i, xi, yo):
        o, upper = chunks[i]
        begin = jnp.where(xi == 0, bounds[o, 0][0], bounds[o, 1][0])
        end = jnp.where(xi == 0, bounds[o, 0][1], bounds[o, 1][1])
        return cum[begin, yo, c, span(upper), lanes(0)] - cum[end, yo, c, span(upper), lanes(0)]

    def top_part(o, xi, yo, side):
        begin, end = bounds[o + zn - 2, xi]
        return cum[begin, yo, side, span(0)] - cum[end, yo, side, span(0)]

    def remote(src, dst, send, recv, peer):
        copy = pltpu.make_async_remote_copy(
            src_ref=src, dst_ref=dst, send_sem=send, recv_sem=recv, device_id=peer, device_id_type=MESH
        )
        copy.start()

    def settle(ref, sem):
        local(ref, ref, sem).wait()

    def stage0(o):
        for xi in range(2):
            for yo in range(yn):
                for h in range(2):
                    send0[o, h, xi, yo] = part(o, h, xi, yo, 1 - c)
        if o == 0:
            pl.semaphore_wait(barrier, len(near) + n_line)
        remote(send0.at[o], recv0.at[o], s0, r0.at[o], core_peer)

    def stage1(o):
        settle(recv0.at[o], r0.at[o])
        for yo in range(yn):
            send1[o, yo] = own_part(o, 1 - x, yo) + recv0[o, 0, 1 - x, yo]
        block = pl.ds(0, yn)
        remote(send1.at[o, block], recv1.at[o, block], s1, r1.at[o], x_peer)
        for i, yo in enumerate(y_ids):
            for xi in range(2):
                send1[o, yn + 2 * i + xi] = part(o, 1, xi, yo, c) + recv0[o, 1, xi, yo]
            block = pl.ds(yn + 2 * i, 2)
            remote(send1.at[o, block], recv1.at[o, block], s1, r1.at[o], y_peers[i])

    def stage2(o):
        settle(recv1.at[o], r1.at[o])
        for yo in range(yn):
            sum2a[o, yo] = own_part(o, x, yo) + recv0[o, 0, x, yo] + recv1[o, yo]
        plane, upper = chunks[o]
        if o < n_far:
            zc = z - lax.rem(z, 2) + lax.rem(order[plane], 2)
            apart = zc != z
            dest, sem = frecv2.at[seat[plane], upper], fr2.at[seat[plane], upper]
            base = jnp.where(apart, yn, 0)
        else:
            zc, dest, sem, base = z, recv2.at[o - n_far], r2.at[o - n_far], 0
        send_sem = fs2 if o < n_far else s2

        def crossing(copy):
            if o < n_far:

                @pl.when(apart)
                def _():
                    copy()

        for d in range(1, yn):
            yo = lax.rem(y + d, yn)
            remote(sum2a.at[o, yo], dest.at[base + d - 1], send_sem, sem, dev(yo, c, zc, x))
        crossing(lambda: remote(sum2a.at[o, y], dest.at[2 * yn], send_sem, sem, dev(y, c, zc, x)))
        for xi in range(2):
            total = part(o, 1, xi, y, c) + recv0[o, 1, xi, y]
            for i in range(yn - 1):
                total = total + recv1[o, yn + 2 * i + xi]
            sum2b[o, xi] = total
        remote(sum2b.at[o, 1 - x], dest.at[base + yn - 1], send_sem, sem, dev(y, c, zc, 1 - x))
        crossing(lambda: remote(sum2b.at[o, x], dest.at[2 * yn + 1], send_sem, sem, dev(y, c, zc, x)))

    def collect(e, upper):
        settle(frecv2.at[e, upper], fr2.at[e, upper])
        i = place[e] * 2 + upper
        total = sum2a[i, y] + frecv2[e, upper, 2 * yn]
        for d in list(range(yn - 1)) + list(range(yn, 2 * yn - 1)):
            total = total + frecv2[e, upper, d]
        j = 2 * e + upper
        sum3[j, 0] = total
        sum3[j, 1] = sum2b[i, x] + frecv2[e, upper, yn - 1] + frecv2[e, upper, 2 * yn - 1] + frecv2[e, upper, 2 * yn + 1]
        pair, there = lax.div(z, 2), lax.div(goal[e], 2)
        slot = (pair - (pair > there).astype(jnp.int32)) * 2 + upper
        remote(sum3.at[j], recv3.at[slot], s3, r3, dev(y, c, goal[e], x))

    def stage3(i):
        settle(recv2.at[i], r2.at[i])
        o, j = n_far + i, 2 * kept + i
        total = sum2a[o, y]
        for k in range(yn - 1):
            total = total + recv2[i, k]
        sum3[j, 0] = total
        sum3[j, 1] = sum2b[o, x] + recv2[i, yn - 1]
        if i == 0:
            remote(sum3.at[j], recv3.at[2 * kept], s3, r3, mate)

    def top_stage0():
        for i in range(2):
            for xi in range(2):
                for yo in range(yn):
                    tsend0[i, xi, yo] = top_part(i, xi, yo, 1 - c)
        remote(tsend0, trecv0, top_sem.at[0], top_sem.at[1], core_peer)

    def top_stage1():
        settle(trecv0, top_sem.at[1])
        for xi in range(2):
            for yo in range(yn):
                tsend1[xi, yo] = top_part(0, xi, yo, c) + trecv0[0, xi, yo]
        remote(tsend1, trecv1, top_sem.at[2], top_sem.at[3], mate)

    def top_stage2():
        settle(trecv1, top_sem.at[3])
        for xi in range(2):
            for yo in range(yn):
                tsum[xi, yo] = top_part(1, xi, yo, c) + trecv0[1, xi, yo] + trecv1[xi, yo]
        for dx in range(2):
            for dy in range(yn):
                if dx or dy:
                    xo, yo = lax.rem(x + dx, 2), lax.rem(y + dy, yn)
                    i = dx * yn + dy - 1
                    remote(tsum.at[xo, yo], trecv2.at[i], top_sem.at[4], top_sem.at[5], dev(yo, c, z, xo))

    n = len(chunks)
    prefix(1 - c)
    stage0(0)
    if zn > 2:
        greet(relay.at[0])
    stage0(1)
    top_stage0()
    for o in range(2, n):
        stage0(o)
    prefix(c)
    stage1(0)
    stage1(1)
    top_stage1()
    for o in range(2, n - HOLD):
        stage1(o)
    for r in range(zn - 3):
        pl.semaphore_wait(relay.at[r], n_line)
        greet(relay.at[r + 1])
    for o in range(HOLD):
        stage2(o)
        stage1(n - HOLD + o)
    for o in range(HOLD, n):
        if o == T2:
            top_stage2()
        stage2(o)
    if T2 >= n:
        top_stage2()
    if zn > 2:
        pl.semaphore_wait(relay.at[zn - 3], n_line)
    for e in range(kept):
        for upper in range(2):
            collect(e, upper)
    stage3(0)
    stage3(1)

    settle(trecv2, top_sem.at[5])
    total = tsum[x, y]
    for i in range(2 * yn - 1):
        total = total + trecv2[i]
    settle(recv3, r3)
    for h in range(2):
        part0 = total[:, lanes(h)]
        part1 = sum3[2 * kept + 1, h] + recv3[2 * kept, h]
        for i in range(kept):
            part0 = part0 + recv3[2 * i, h]
            part1 = part1 + recv3[2 * i + 1, h]
        out[0, span(0), lanes(h)] = part0
        out[0, span(1), lanes(h)] = part1
    settle(tsend0, top_sem.at[0])
    settle(tsend1, top_sem.at[2])
    settle(trecv2, top_sem.at[4])
    settle(send0, s0)
    settle(send1, s1)
    settle(recv2, s2)
    settle(frecv2, fs2)
    settle(recv3, s3)


def on_device(lhat, ainv, diag, targets):
    rows, cols = lax.axis_size("row"), lax.axis_size("col")
    slots, width = lhat.shape[0], lhat.shape[2]
    height = lhat.shape[1]
    yn, zn, share = rows // 2, cols // 2, diag.shape[1]
    half = width // 2
    f32, dma = jnp.float32, pltpu.SemaphoreType.DMA
    n, kept = 2 * zn - 2, zn // 2 - 1
    low, high = (share // 2, half), (share // 2, width)
    scratch = [
        pltpu.SMEM((1, slots), jnp.int32),
        pltpu.VMEM((slots, height, width), f32),
        pltpu.VMEM((slots, height, width), f32),
        pltpu.VMEM((share, width), f32),
        pltpu.VMEM((slots + 1, yn, 2, share, width), f32),
        pltpu.VMEM((slots + 2, yn, 2, share, width), f32),
        pltpu.VMEM((n, 2, 2, yn) + low, f32),
        pltpu.VMEM((n, 2, 2, yn) + low, f32),
        pltpu.VMEM((n, 3 * yn - 2) + low, f32),
        pltpu.VMEM((n, 3 * yn - 2) + low, f32),
        pltpu.VMEM((n, yn) + low, f32),
        pltpu.VMEM((n, 2) + low, f32),
        pltpu.VMEM((2, yn) + low, f32),
        pltpu.VMEM((kept, 2, 2 * yn + 2) + low, f32),
        pltpu.VMEM((2 * kept + 2, 2) + low, f32),
        pltpu.VMEM((2 * kept + 1, 2) + low, f32),
        pltpu.VMEM((2, 2, yn) + high, f32),
        pltpu.VMEM((2, 2, yn) + high, f32),
        pltpu.VMEM((2, yn) + high, f32),
        pltpu.VMEM((2, yn) + high, f32),
        pltpu.VMEM((2, yn) + high, f32),
        pltpu.VMEM((2 * yn - 1,) + high, f32),
        dma((5,)), pltpu.SemaphoreType.REGULAR((max(zn - 2, 1),)),
        dma, dma((n,)), dma, dma((n,)), dma, dma((2,)), dma, dma((kept, 2)), dma, dma, dma((6,)),
    ]
    return pl.pallas_call(
        functools.partial(kernel, (yn, zn, slots, share, width)),
        out_shape=pltpu.VMEM(diag.shape, f32),
        in_specs=[pl.BlockSpec(memory_space=pltpu.HBM)] * 4,
        out_specs=pl.BlockSpec(memory_space=pltpu.VMEM),
        scratch_shapes=scratch,
        compiler_params=pltpu.CompilerParams(
            collective_id=0, has_side_effects=True, vmem_limit_bytes=60 * 1024 * 1024
        ),
    )(lhat, ainv, diag, targets.T)


def solution(mesh):
    placed = (
        P(("row", "col"), None, None),
        P(("row", "col"), None, None),
        P("col", "row", None),
        P(("row", "col"), None),
    )
    return jax.shard_map(
        on_device, mesh=mesh, in_specs=placed, out_specs=P("col", "row", None), check_vma=False
    )
```

time: 21.7 us -> 21.2 us (0.977)
  Pallas kernels: 20.9 us -> 20.4 us
    pallas_call x1, Pallas kernels: 20.9 us -> 20.4 us  [on_device(): pl.pallas_call(functools.partial(kernel, (yn, zn, slots, share, width)),...]
where the time goes in v4:
time: 21.2 us; the launch traced here: 21 us
  Pallas kernels  20.4 us (96%)
  local copies, waits for them, and re-layouts  0.63 us (3%)
    pallas_call x1, Pallas kernels, on_device(): pl.pallas_call(functools.partial(kernel, (yn, zn, slots, share, width)),...  20.4 us
    unnamed x1, local copies, waits for them, and re-layouts  0.63 us

profile of v4, /device:TPU:0, one launch (start us, length us, event | category | flops | bytes accessed | tf_op | source)
XLA Modules:
  0.0 21.0 jit_solution(2366674057894283833)
XLA Ops:
  0.0 20.4 %shard_map.46 = f32[1,64,256]{2,1,0:T(8,128)S(1)} custom-call(f32[8,256,256]{2,1,0:T(8,128)} %lhat.1, f32[8,256,256]{2,1,0:T(8,128)} %ainv.1, f32[1,64,256]{2,1,0:T(8,128)} %diag.1, s32[1,8]{1,0:T(1,128)} %bitcast.1), custom_call_target="tpu_custom_call" | custom-call | tf_op jit(solution)/shard_map/pallas_call | solution.py:372
  20.4 0.6 %copy.6 = f32[1,64,256]{2,1,0:T(8,128)} copy(f32[1,64,256]{2,1,0:T(8,128)S(1)} %shard_map.46) | data formatting | bytes 131072

commit v5 on v4

--- a/solution.py
+++ b/solution.py
@@ -23,13 +23,18 @@
     return lax.dot_general(left, right, DN, preferred_element_type=jnp.float32)
 
 
+def dot_groups(slots):
+    cuts = sorted({min(slots, cut) for cut in (0, 1, 4)} | {slots})
+    return list(zip(cuts, cuts[1:]))
+
+
 def kernel(
     dims,
     lhat, ainv, diag, targets_in, out,
     targets, lbuf, abuf, dbuf, prod, cum,
     send0, recv0, send1, recv1, sum2a, sum2b, recv2, frecv2, sum3, recv3,
     tsend0, trecv0, tsend1, trecv1, tsum, trecv2,
-    load_sem, relay, s0, r0, s1, r1, s2, r2, fs2, fr2, s3, r3, top_sem,
+    load_sem, relay, cross, s0, r0, s1, r1, s2, r2, fs2, fr2, s3, r3, top_sem,
 ):
     yn, zn, slots, share, width = dims
     half = width // 2
@@ -80,22 +85,31 @@
     t_load.start()
     d_load = local(diag.at[0], dbuf, load_sem.at[1])
     d_load.start()
-    for s in range(slots):
-        first = s == 0
-        local(lhat.at[s], lbuf.at[s], load_sem.at[2 if first else 3]).start()
-        local(ainv.at[s], abuf.at[s], load_sem.at[2 if first else 4]).start()
+    groups = dot_groups(slots)
+    for g, (first, last) in enumerate(groups):
+        for s in range(first, last):
+            local(lhat.at[s], lbuf.at[s], load_sem.at[2 + 2 * g]).start()
+            local(ainv.at[s], abuf.at[s], load_sem.at[3 + 2 * g]).start()
 
     barrier = pltpu.get_barrier_semaphore()
     for peer in near:
         pl.semaphore_signal(barrier, inc=1, device_id=peer, device_id_type=MESH)
     greet(barrier)
 
-    pair = lbuf.at[pl.ds(0, 2)]
-    local(pair, pair, load_sem.at[2]).wait()
-    prod[0] = gram_dot(lbuf[0], abuf[0]).reshape(yn, 2, share, width)
-    rest = pl.ds(1, slots - 1)
-    local(lhat.at[rest], lbuf.at[rest], load_sem.at[3]).wait()
-    local(ainv.at[rest], abuf.at[rest], load_sem.at[4]).wait()
+    def loaded(g):
+        first, last = groups[g]
+        part = pl.ds(first, last - first)
+        local(lhat.at[part], lbuf.at[part], load_sem.at[2 + 2 * g]).wait()
+        local(ainv.at[part], abuf.at[part], load_sem.at[3 + 2 * g]).wait()
+
+    def multiply(g):
+        for s in range(*groups[g]):
+            prod[s] = gram_dot(lbuf[s], abuf[s]).reshape(yn, 2, share, width)
+
+    for g in range(len(groups) - 1):
+        loaded(g)
+        multiply(g)
+    loaded(len(groups) - 1)
     d_load.wait()
     t_load.wait()
 
@@ -123,8 +137,7 @@
             slot = slot + jnp.where(ranks[s] == j, s, 0)
         sorted_slots.append(slot)
 
-    for s in range(1, slots):
-        prod[s] = gram_dot(lbuf[s], abuf[s]).reshape(yn, 2, share, width)
+    multiply(len(groups) - 1)
     prod[slots] = -gram_dot(dbuf[...], dbuf[...]).reshape(yn, 2, share, width)
 
     def prefix(side):
@@ -148,6 +161,9 @@
     def span(h):
         return slice(h * rows, (h + 1) * rows)
 
+    def side_of(i):
+        return 1 - c if i < n_far else c
+
     def part(i, h, xi, yo, side):
         o, upper = chunks[i]
         begin, end = bounds[o, xi]
@@ -157,7 +173,8 @@
         o, upper = chunks[i]
         begin = jnp.where(xi == 0, bounds[o, 0][0], bounds[o, 1][0])
         end = jnp.where(xi == 0, bounds[o, 0][1], bounds[o, 1][1])
-        return cum[begin, yo, c, span(upper), lanes(0)] - cum[end, yo, c, span(upper), lanes(0)]
+        side = side_of(i)
+        return cum[begin, yo, side, span(upper), lanes(0)] - cum[end, yo, side, span(upper), lanes(0)]
 
     def top_part(o, xi, yo, side):
         begin, end = bounds[o + zn - 2, xi]
@@ -176,7 +193,7 @@
         for xi in range(2):
             for yo in range(yn):
                 for h in range(2):
-                    send0[o, h, xi, yo] = part(o, h, xi, yo, 1 - c)
+                    send0[o, h, xi, yo] = part(o, h, xi, yo, 1 - side_of(o))
         if o == 0:
             pl.semaphore_wait(barrier, len(near) + n_line)
         remote(send0.at[o], recv0.at[o], s0, r0.at[o], core_peer)
@@ -189,7 +206,7 @@
         remote(send1.at[o, block], recv1.at[o, block], s1, r1.at[o], x_peer)
         for i, yo in enumerate(y_ids):
             for xi in range(2):
-                send1[o, yn + 2 * i + xi] = part(o, 1, xi, yo, c) + recv0[o, 1, xi, yo]
+                send1[o, yn + 2 * i + xi] = part(o, 1, xi, yo, side_of(o)) + recv0[o, 1, xi, yo]
             block = pl.ds(yn + 2 * i, 2)
             remote(send1.at[o, block], recv1.at[o, block], s1, r1.at[o], y_peers[i])
 
@@ -219,7 +236,7 @@
             remote(sum2a.at[o, yo], dest.at[base + d - 1], send_sem, sem, dev(yo, c, zc, x))
         crossing(lambda: remote(sum2a.at[o, y], dest.at[2 * yn], send_sem, sem, dev(y, c, zc, x)))
         for xi in range(2):
-            total = part(o, 1, xi, y, c) + recv0[o, 1, xi, y]
+            total = part(o, 1, xi, y, side_of(o)) + recv0[o, 1, xi, y]
             for i in range(yn - 1):
                 total = total + recv1[o, yn + 2 * i + xi]
             sum2b[o, xi] = total
@@ -237,7 +254,7 @@
         sum3[j, 1] = sum2b[i, x] + frecv2[e, upper, yn - 1] + frecv2[e, upper, 2 * yn - 1] + frecv2[e, upper, 2 * yn + 1]
         pair, there = lax.div(z, 2), lax.div(goal[e], 2)
         slot = (pair - (pair > there).astype(jnp.int32)) * 2 + upper
-        remote(sum3.at[j], recv3.at[slot], s3, r3, dev(y, c, goal[e], x))
+        remote(sum3.at[j], recv3.at[slot], s3, r3, dev(y, 1 - c, goal[e], x))
 
     def stage3(i):
         settle(recv2.at[i], r2.at[i])
@@ -277,15 +294,15 @@
                     remote(tsum.at[xo, yo], trecv2.at[i], top_sem.at[4], top_sem.at[5], dev(yo, c, z, xo))
 
     n = len(chunks)
-    prefix(1 - c)
+    prefix(c)
     stage0(0)
     if zn > 2:
         greet(relay.at[0])
     stage0(1)
+    prefix(1 - c)
     top_stage0()
     for o in range(2, n):
         stage0(o)
-    prefix(c)
     stage1(0)
     stage1(1)
     top_stage1()
@@ -305,6 +322,8 @@
         top_stage2()
     if zn > 2:
         pl.semaphore_wait(relay.at[zn - 3], n_line)
+        pl.semaphore_signal(cross, inc=1, device_id=core_peer, device_id_type=MESH)
+        pl.semaphore_wait(cross, 1)
     for e in range(kept):
         for upper in range(2):
             collect(e, upper)
@@ -366,8 +385,8 @@
         pltpu.VMEM((2, yn) + high, f32),
         pltpu.VMEM((2, yn) + high, f32),
         pltpu.VMEM((2 * yn - 1,) + high, f32),
-        dma((5,)), pltpu.SemaphoreType.REGULAR((max(zn - 2, 1),)),
-        dma, dma((n,)), dma, dma((n,)), dma, dma((2,)), dma, dma((kept, 2)), dma, dma, dma((6,)),
+        dma((2 + 2 * len(dot_groups(slots)),)), pltpu.SemaphoreType.REGULAR((max(zn - 2, 1),)),
+        pltpu.SemaphoreType.REGULAR, dma, dma((n,)), dma, dma((n,)), dma, dma((2,)), dma, dma((kept, 2)), dma, dma, dma((6,)),
     ]
     return pl.pallas_call(
         functools.partial(kernel, (yn, zn, slots, share, width)),

time: 21.2 us -> 20.3 us (0.958)
  Pallas kernels: 20.4 us -> 19.5 us
    pallas_call x1, Pallas kernels: 20.4 us -> 19.5 us  [on_device(): pl.pallas_call(functools.partial(kernel, (yn, zn, slots, share, width)),...]
where the time goes in v5:
time: 20.3 us; the launch traced here: 20.2 us
  Pallas kernels  19.5 us (96%)
  local copies, waits for them, and re-layouts  0.63 us (3%)
    pallas_call x1, Pallas kernels, on_device(): pl.pallas_call(functools.partial(kernel, (yn, zn, slots, share, width)),...  19.5 us
    unnamed x1, local copies, waits for them, and re-layouts  0.63 us

profile of v5, /device:TPU:0, one launch (start us, length us, event | category | flops | bytes accessed | tf_op | source)
XLA Modules:
  0.0 20.2 jit_solution(9320364234768249392)
XLA Ops:
  0.0 19.5 %shard_map.46 = f32[1,64,256]{2,1,0:T(8,128)S(1)} custom-call(f32[8,256,256]{2,1,0:T(8,128)} %lhat.1, f32[8,256,256]{2,1,0:T(8,128)} %ainv.1, f32[1,64,256]{2,1,0:T(8,128)} %diag.1, s32[1,8]{1,0:T(1,128)} %bitcast.1), custom_call_target="tpu_custom_call" | custom-call | tf_op jit(solution)/shard_map/pallas_call | solution.py:391
  19.5 0.6 %copy.6 = f32[1,64,256]{2,1,0:T(8,128)} copy(f32[1,64,256]{2,1,0:T(8,128)S(1)} %shard_map.46) | data formatting | bytes 131072

commit v6 on v5

--- a/solution.py
+++ b/solution.py
@@ -54,11 +54,9 @@
 
     far = [[d for d in [0] + list(range(zn - 1, 0, -1)) if d // 2 != q // 2] for q in range(zn)]
     order = [by_plane([far[q][o] for q in range(zn)]) for o in range(zn - 2)] + [z + 1 - 2 * lax.rem(z, 2), z]
-    seat = [by_plane([[d for d in far[q] if d % 2 == far[q][o] % 2].index(far[q][o]) for q in range(zn)]) for o in range(zn - 2)]
+    mirrored = z >= zn // 2
+    kept_half = jnp.where(mirrored, 1 - lax.rem(z, 2), lax.rem(z, 2))
     kept = zn // 2 - 1
-    mine = [[[o for o, d in enumerate(far[q]) if d % 2 == q % 2][e] for q in range(zn)] for e in range(kept)]
-    place = [by_plane(mine[e]) for e in range(kept)]
-    goal = [by_plane([far[q][mine[e][q]] for q in range(zn)]) for e in range(kept)]
     chunks = [(o, h) for o in range(zn - 2) for h in range(2)] + [(zn - 2, 1), (zn - 1, 1)]
     n_far = 2 * (zn - 2)
     core_peer = dev(y, 1 - c, z, x)
@@ -66,6 +64,7 @@
     y_ids = [lax.rem(y + d, yn) for d in range(1, yn)]
     y_peers = [dev(i, c, z, x) for i in y_ids]
     mate = dev(y, c, z + 1 - 2 * lax.rem(z, 2), x)
+    twin = dev(y, 1 - c, z + 1 - 2 * lax.rem(z, 2), x)
     below, above = z > 0, z < zn - 1
     line = [(below, dev(y, c, z - 1, x)), (above, dev(y, c, z + 1, x))]
     n_line = below.astype(jnp.int32) + above.astype(jnp.int32)
@@ -162,7 +161,7 @@
         return slice(h * rows, (h + 1) * rows)
 
     def side_of(i):
-        return 1 - c if i < n_far else c
+        return 1 - c if i <= n_far else c
 
     def part(i, h, xi, yo, side):
         o, upper = chunks[i]
@@ -216,9 +215,9 @@
             sum2a[o, yo] = own_part(o, x, yo) + recv0[o, 0, x, yo] + recv1[o, yo]
         plane, upper = chunks[o]
         if o < n_far:
-            zc = z - lax.rem(z, 2) + lax.rem(order[plane], 2)
+            zc = z - lax.rem(z, 2) + jnp.where(mirrored, 1 - upper, upper)
             apart = zc != z
-            dest, sem = frecv2.at[seat[plane], upper], fr2.at[seat[plane], upper]
+            dest, sem = frecv2.at[plane], fr2.at[plane]
             base = jnp.where(apart, yn, 0)
         else:
             zc, dest, sem, base = z, recv2.at[o - n_far], r2.at[o - n_far], 0
@@ -243,18 +242,17 @@
         remote(sum2b.at[o, 1 - x], dest.at[base + yn - 1], send_sem, sem, dev(y, c, zc, 1 - x))
         crossing(lambda: remote(sum2b.at[o, x], dest.at[2 * yn + 1], send_sem, sem, dev(y, c, zc, x)))
 
-    def collect(e, upper):
-        settle(frecv2.at[e, upper], fr2.at[e, upper])
-        i = place[e] * 2 + upper
-        total = sum2a[i, y] + frecv2[e, upper, 2 * yn]
+    def collect(e):
+        settle(frecv2.at[e], fr2.at[e])
+        i = e * 2 + kept_half
+        total = sum2a[i, y] + frecv2[e, 2 * yn]
         for d in list(range(yn - 1)) + list(range(yn, 2 * yn - 1)):
-            total = total + frecv2[e, upper, d]
-        j = 2 * e + upper
-        sum3[j, 0] = total
-        sum3[j, 1] = sum2b[i, x] + frecv2[e, upper, yn - 1] + frecv2[e, upper, 2 * yn - 1] + frecv2[e, upper, 2 * yn + 1]
-        pair, there = lax.div(z, 2), lax.div(goal[e], 2)
-        slot = (pair - (pair > there).astype(jnp.int32)) * 2 + upper
-        remote(sum3.at[j], recv3.at[slot], s3, r3, dev(y, 1 - c, goal[e], x))
+            total = total + frecv2[e, d]
+        sum3[e, 0] = total
+        sum3[e, 1] = sum2b[i, x] + frecv2[e, yn - 1] + frecv2[e, 2 * yn - 1] + frecv2[e, 2 * yn + 1]
+        pair, there = lax.div(z, 2), lax.div(order[e], 2)
+        slot = (pair - (pair > there).astype(jnp.int32)) * 2 + kept_half
+        remote(sum3.at[e], recv3.at[slot], s3, r3, dev(y, 1 - c, order[e], x))
 
     def stage3(i):
         settle(recv2.at[i], r2.at[i])
@@ -265,7 +263,7 @@
         sum3[j, 0] = total
         sum3[j, 1] = sum2b[o, x] + recv2[i, yn - 1]
         if i == 0:
-            remote(sum3.at[j], recv3.at[2 * kept], s3, r3, mate)
+            remote(sum3.at[j], recv3.at[2 * kept], s3, r3, twin)
 
     def top_stage0():
         for i in range(2):
@@ -315,18 +313,16 @@
         stage2(o)
         stage1(n - HOLD + o)
     for o in range(HOLD, n):
-        if o == T2:
-            top_stage2()
+        if o == 2:
+            pl.semaphore_wait(relay.at[zn - 3], n_line)
+            pl.semaphore_signal(cross, inc=1, device_id=core_peer, device_id_type=MESH)
+        if o == n - 1:
+            pl.semaphore_wait(cross, 1)
+            collect(0)
         stage2(o)
-    if T2 >= n:
-        top_stage2()
-    if zn > 2:
-        pl.semaphore_wait(relay.at[zn - 3], n_line)
-        pl.semaphore_signal(cross, inc=1, device_id=core_peer, device_id_type=MESH)
-        pl.semaphore_wait(cross, 1)
-    for e in range(kept):
-        for upper in range(2):
-            collect(e, upper)
+    top_stage2()
+    for e in range(1, zn - 2):
+        collect(e)
     stage3(0)
     stage3(1)
 
@@ -376,7 +372,7 @@
         pltpu.VMEM((n, yn) + low, f32),
         pltpu.VMEM((n, 2) + low, f32),
         pltpu.VMEM((2, yn) + low, f32),
-        pltpu.VMEM((kept, 2, 2 * yn + 2) + low, f32),
+        pltpu.VMEM((zn - 2, 2 * yn + 2) + low, f32),
         pltpu.VMEM((2 * kept + 2, 2) + low, f32),
         pltpu.VMEM((2 * kept + 1, 2) + low, f32),
         pltpu.VMEM((2, 2, yn) + high, f32),
@@ -386,7 +382,7 @@
         pltpu.VMEM((2, yn) + high, f32),
         pltpu.VMEM((2 * yn - 1,) + high, f32),
         dma((2 + 2 * len(dot_groups(slots)),)), pltpu.SemaphoreType.REGULAR((max(zn - 2, 1),)),
-        pltpu.SemaphoreType.REGULAR, dma, dma((n,)), dma, dma((n,)), dma, dma((2,)), dma, dma((kept, 2)), dma, dma, dma((6,)),
+        pltpu.SemaphoreType.REGULAR, dma, dma((n,)), dma, dma((n,)), dma, dma((2,)), dma, dma((zn - 2,)), dma, dma, dma((6,)),
     ]
     return pl.pallas_call(
         functools.partial(kernel, (yn, zn, slots, share, width)),

time: 20.3 us -> 19.9 us (0.980)
  the two profiles are of different devices: /device:TPU:0 before, /device:TPU:1 now
where the time goes in v6:
time: 19.9 us; the launch traced here: 19.8 us
  Pallas kernels  19.1 us (96%)
  local copies, waits for them, and re-layouts  0.63 us (3%)
    pallas_call x1, Pallas kernels, on_device(): pl.pallas_call(functools.partial(kernel, (yn, zn, slots, share, width)),...  19.1 us
    unnamed x1, local copies, waits for them, and re-layouts  0.63 us

profile of v6, /device:TPU:1, one launch (start us, length us, event | category | flops | bytes accessed | tf_op | source)
XLA Modules:
  0.0 19.8 jit_solution(7508209697218089661)
XLA Ops:
  0.0 19.1 %shard_map.46 = f32[1,64,256]{2,1,0:T(8,128)S(1)} custom-call(f32[8,256,256]{2,1,0:T(8,128)} %lhat.1, f32[8,256,256]{2,1,0:T(8,128)} %ainv.1, f32[1,64,256]{2,1,0:T(8,128)} %diag.1, s32[1,8]{1,0:T(1,128)} %bitcast.1), custom_call_target="tpu_custom_call" | custom-call | tf_op jit(solution)/shard_map/pallas_call | solution.py:387
  19.1 0.6 %copy.6 = f32[1,64,256]{2,1,0:T(8,128)} copy(f32[1,64,256]{2,1,0:T(8,128)S(1)} %shard_map.46) | data formatting | bytes 131072

commit v7 on v6

--- a/solution.py
+++ b/solution.py
@@ -105,10 +105,7 @@
         for s in range(*groups[g]):
             prod[s] = gram_dot(lbuf[s], abuf[s]).reshape(yn, 2, share, width)
 
-    for g in range(len(groups) - 1):
-        loaded(g)
-        multiply(g)
-    loaded(len(groups) - 1)
+    loaded(0)
     d_load.wait()
     t_load.wait()
 
@@ -136,8 +133,13 @@
             slot = slot + jnp.where(ranks[s] == j, s, 0)
         sorted_slots.append(slot)
 
+    multiply(0)
+    prod[slots] = -gram_dot(dbuf[...], dbuf[...]).reshape(yn, 2, share, width)
+    for g in range(1, len(groups) - 1):
+        loaded(g)
+        multiply(g)
+    loaded(len(groups) - 1)
     multiply(len(groups) - 1)
-    prod[slots] = -gram_dot(dbuf[...], dbuf[...]).reshape(yn, 2, share, width)
 
     def prefix(side):
         for yo in range(yn):
@@ -318,12 +320,30 @@
             pl.semaphore_signal(cross, inc=1, device_id=core_peer, device_id_type=MESH)
         if o == n - 1:
             pl.semaphore_wait(cross, 1)
-            collect(0)
+
+            @pl.when(mirrored)
+            def _():
+                collect(0)
+
         stage2(o)
     top_stage2()
-    for e in range(1, zn - 2):
-        collect(e)
+
+    @pl.when(jnp.logical_not(mirrored))
+    def _():
+        collect(0)
+
+    @pl.when(mirrored)
+    def _():
+        for e in range(1, zn - 2):
+            collect(e)
+
     stage3(0)
+
+    @pl.when(jnp.logical_not(mirrored))
+    def _():
+        for e in range(1, zn - 2):
+            collect(e)
+
     stage3(1)
 
     settle(trecv2, top_sem.at[5])

time: 19.9 us -> 19.9 us (level)
  no operation moved by 1% of the time
where the time goes in v7:
time: 19.9 us; the launch traced here: 19.7 us
  Pallas kernels  19.1 us (96%)
  local copies, waits for them, and re-layouts  0.63 us (3%)
    pallas_call x1, Pallas kernels, on_device(): pl.pallas_call(functools.partial(kernel, (yn, zn, slots, share, width)),...  19.1 us
    unnamed x1, local copies, waits for them, and re-layouts  0.63 us

profile of v7, /device:TPU:1, one launch (start us, length us, event | category | flops | bytes accessed | tf_op | source)
XLA Modules:
  0.0 19.7 jit_solution(6767139055872250252)
XLA Ops:
  0.0 19.1 %shard_map.46 = f32[1,64,256]{2,1,0:T(8,128)S(1)} custom-call(f32[8,256,256]{2,1,0:T(8,128)} %lhat.1, f32[8,256,256]{2,1,0:T(8,128)} %ainv.1, f32[1,64,256]{2,1,0:T(8,128)} %diag.1, s32[1,8]{1,0:T(1,128)} %bitcast.1), custom_call_target="tpu_custom_call" | custom-call | tf_op jit(solution)/shard_map/pallas_call | solution.py:407
  19.1 0.6 %copy.6 = f32[1,64,256]{2,1,0:T(8,128)} copy(f32[1,64,256]{2,1,0:T(8,128)S(1)} %shard_map.46) | data formatting | bytes 131072

commit v8 on v7

--- a/solution.py
+++ b/solution.py
@@ -87,8 +87,8 @@
     groups = dot_groups(slots)
     for g, (first, last) in enumerate(groups):
         for s in range(first, last):
-            local(lhat.at[s], lbuf.at[s], load_sem.at[2 + 2 * g]).start()
-            local(ainv.at[s], abuf.at[s], load_sem.at[3 + 2 * g]).start()
+            local(lhat.at[s], lbuf.at[s], load_sem.at[2 + g]).start()
+            local(ainv.at[s], abuf.at[s], load_sem.at[2 + g]).start()
 
     barrier = pltpu.get_barrier_semaphore()
     for peer in near:
@@ -97,9 +97,8 @@
 
     def loaded(g):
         first, last = groups[g]
-        part = pl.ds(first, last - first)
-        local(lhat.at[part], lbuf.at[part], load_sem.at[2 + 2 * g]).wait()
-        local(ainv.at[part], abuf.at[part], load_sem.at[3 + 2 * g]).wait()
+        both = lbuf.at[pl.ds(0, 2 * (last - first))]
+        local(both, both, load_sem.at[2 + g]).wait()
 
     def multiply(g):
         for s in range(*groups[g]):
@@ -401,7 +400,7 @@
         pltpu.VMEM((2, yn) + high, f32),
         pltpu.VMEM((2, yn) + high, f32),
         pltpu.VMEM((2 * yn - 1,) + high, f32),
-        dma((2 + 2 * len(dot_groups(slots)),)), pltpu.SemaphoreType.REGULAR((max(zn - 2, 1),)),
+        dma((2 + len(dot_groups(slots)),)), pltpu.SemaphoreType.REGULAR((max(zn - 2, 1),)),
         pltpu.SemaphoreType.REGULAR, dma, dma((n,)), dma, dma((n,)), dma, dma((2,)), dma, dma((zn - 2,)), dma, dma, dma((6,)),
     ]
     return pl.pallas_call(

time: 19.9 us -> 19.8 us (level)
  no operation moved by 1% of the time
where the time goes in v8:
time: 19.8 us; the launch traced here: 19.7 us
  Pallas kernels  19.1 us (96%)
  local copies, waits for them, and re-layouts  0.63 us (3%)
    pallas_call x1, Pallas kernels, on_device(): pl.pallas_call(functools.partial(kernel, (yn, zn, slots, share, width)),...  19.1 us
    unnamed x1, local copies, waits for them, and re-layouts  0.63 us

profile of v8, /device:TPU:1, one launch (start us, length us, event | category | flops | bytes accessed | tf_op | source)
XLA Modules:
  0.0 19.7 jit_solution(4888563632704798570)
XLA Ops:
  0.0 19.1 %shard_map.46 = f32[1,64,256]{2,1,0:T(8,128)S(1)} custom-call(f32[8,256,256]{2,1,0:T(8,128)} %lhat.1, f32[8,256,256]{2,1,0:T(8,128)} %ainv.1, f32[1,64,256]{2,1,0:T(8,128)} %diag.1, s32[1,8]{1,0:T(1,128)} %bitcast.1), custom_call_target="tpu_custom_call" | custom-call | tf_op jit(solution)/shard_map/pallas_call | solution.py:406
  19.1 0.6 %copy.6 = f32[1,64,256]{2,1,0:T(8,128)} copy(f32[1,64,256]{2,1,0:T(8,128)S(1)} %shard_map.46) | data formatting | bytes 131072
